TPU v7x, 32 devices: a whole 2x2x4 slice. The times are simulated.
32 devices in a mesh: gx: 8 (over z, y), gy: 4 (over x, core).
Axes of the slice: x: 2, y: 2, z: 4, core: 2. Of those that a mesh axis runs over, the one named last changes fastest.
Arguments:
- three_index: bfloat16 [8, 4608, 4608], P('gx', 'gy'), as said below
- old_density: bfloat16 [4608, 4608], P('gy'), as said below
- core: float32 [4608, 4608], P('gy', 'gx'), as said below
Outputs:
- purified: bfloat16 [4608, 4608], P('gy', 'gx')
- idempotency: float32 [2], replicated
Inputs may be any that keep to these rules, and one draw needn't show every extreme that they name: Each slab three_index[P] is symmetric in its two basis indices. `old_density`: symmetric. `core`: symmetric.
All inputs are finite; a program needn't handle non-finite values.
Results may differ from a plain program's by a relative error of at most 0.015.
Values may be sent and summed in bfloat16 or wider, within the bound.
A program may use at most 128 MiB of HBM per device.

v0:
```python
import jax
import jax.numpy as jnp
from jax import lax
from jax.sharding import PartitionSpec as P

ITERS = 2


def per_device(three_index, old_density, core):
    aux_dev, rows, width = three_index.shape
    cols = core.shape[1]
    flat = three_index.reshape(aux_dev, rows * width)
    partial_value = jnp.dot(
        flat, old_density.reshape(rows * width), preferred_element_type=jnp.float32
    )
    fitted = lax.psum(partial_value, "gy")
    fitted16 = fitted.astype(jnp.bfloat16)
    coulomb = lax.psum_scatter(
        jnp.einsum("p,prc->cr", fitted16, three_index, preferred_element_type=jnp.float32).astype(
            jnp.bfloat16
        ),
        "gx",
        scatter_dimension=0,
        tiled=True,
    ).astype(jnp.float32)
    fock = core + coulomb.T
    row_start = lax.axis_index("gy") * rows
    col_start = lax.axis_index("gx") * cols
    row_ids = row_start + lax.broadcasted_iota(jnp.int32, (rows, cols), 0)
    col_ids = col_start + lax.broadcasted_iota(jnp.int32, (rows, cols), 1)
    diag_mask = (row_ids == col_ids).astype(jnp.float32)
    local_trace = jnp.sum(fock * diag_mask)
    shift = lax.psum(local_trace, ("gx", "gy")) / width
    shifted = fock - shift * diag_mask
    spread = lax.psum(jnp.sum(shifted * shifted), ("gx", "gy")) / (width * width)
    current = ((shift * diag_mask - fock) / (4.0 * jnp.sqrt(spread + 1e-06))).astype(jnp.bfloat16)
    scale = 1.0 / jnp.sqrt(jnp.float32(width))
    traces = []
    for step in range(ITERS):
        right = lax.all_gather(current, "gy", axis=0, tiled=True)
        row_panel = lax.all_gather(current, "gx", axis=1, tiled=True)
        square_full = jnp.dot(row_panel, right, preferred_element_type=jnp.float32) * scale
        square = square_full.astype(jnp.bfloat16)
        square_block = lax.all_gather(square, "gy", axis=0, tiled=True)
        cube = jnp.dot(row_panel, square_block, preferred_element_type=jnp.float32) * scale
        traces.append(jnp.sum(square_full * diag_mask))
        current = (1.5 * current.astype(jnp.float32) - 2.0 * cube).astype(jnp.bfloat16)
    totals = lax.psum(jnp.stack(traces), ("gx", "gy"))
    idempotency = 16.0 * (0.25 - totals / (width * jnp.sqrt(jnp.float32(width))))
    return (current, idempotency)


def solution(mesh):
    placed = (P("gx", "gy", None), P("gy", None), P("gy", "gx"))
    return jax.shard_map(
        per_device, mesh=mesh, in_specs=placed, out_specs=(P("gy", "gx"), P()), check_vma=False
    )
```

profile of v0, /device:TPU:0, one launch (start us, length us, event | category | flops | bytes accessed | tf_op | source)
XLA Modules:
  0.0 895.6 jit_solution(16187595499375123604)
XLA Ops:
  7.2 0.0 reduce-scatter.2.cloned.1.call-start
  7.2 19.8 %reshape.23 = bf16[5308416]{0:T(1024)(128)(2,1)} reshape(bf16[1,1152,4608]{2,1,0:T(8,128)(2,1)} %param.3) | data formatting | bytes 21233664 | tf_op jit(solution)/shard_map/reshape
  27.0 15.3 %copy.5 = bf16[1,1152,4608]{1,2,0:T(8,128)(2,1)} copy(bf16[1,1152,4608]{2,1,0:T(8,128)(2,1)} %param.3) | data formatting | bytes 21233664 | tf_op args[0]
  42.3 19.8 %reshape.24 = bf16[5308416]{0:T(1024)(128)(2,1)} reshape(bf16[1152,4608]{1,0:T(8,128)(2,1)} %param.4) | data formatting | bytes 21233664 | tf_op jit(solution)/shard_map/reshape | solution.py:14
  62.1 10.9 %fusion = f32[]{:T(128)} fusion(bf16[5308416]{0:T(1024)(128)(2,1)} %reshape.23, bf16[5308416]{0:T(1024)(128)(2,1)} %reshape.24), kind=kLoop, calls=%fused_computation.1 | loop fusion | flops 21233664 | bytes 21233668 | tf_op jit(solution)/shard_map/dot_general | solution.py:13
  72.9 9.0 %psum.28 = bf16[1]{0:T(256)(128)(2,1)} all-reduce(f32[1]{0:T(128)} %bitcast), channel_id=1, replica_groups=mesh['gx'=8,'gy'=4] {'gy'}, use_global_device_ids=true, to_apply=%region_0.0 | all-reduce | flops 1 | bytes 6 | tf_op jit(solution)/shard_map/psum | solution.py:16
  82.6 10.5 %fusion.1 = bf16[4608,1152]{1,0:T(8,128)(2,1)} fusion(bf16[1,1152,4608]{1,2,0:T(8,128)(2,1)} %copy.5, f32[]{:T(128)S(6)} %convert.13), kind=kLoop, calls=%fused_computation.3 | loop fusion | flops 15925248 | bytes 21233668 | tf_op jit(solution)/shard_map/convert_element_type | solution.py:19
  93.1 0.0 all-gather.9.cloned.1.call-start
  93.2 180.8 %reduce-scatter.2.cloned.1.call-done = bf16[576,1152]{1,0:T(8,128)(2,1)} async-done(((bf16[4608,1152]{1,0:T(8,128)(2,1)}), bf16[576,1152]{1,0:T(8,128)(2,1)}) %reduce-scatter.2.cloned.1.call-update) | async-done | bytes 1327120 | tf_op jit(solution)/shard_map/reduce_scatter | solution.py:18
  274.1 2.8 fusion.11
  276.9 39.5 %psum.29 = f32[]{:T(128)} all-reduce(f32[]{:T(128)} %fusion.11), channel_id=1, replica_groups=mesh['gx'=8,'gy'=4] {'gx','gy'}, use_global_device_ids=true, to_apply=%region_3.0 | all-reduce | flops 1 | bytes 8 | tf_op jit(solution)/shard_map/psum | solution.py:33
  317.0 2.9 fusion.10
  319.9 40.2 %psum.30 = f32[]{:T(128)} all-reduce(f32[]{:T(128)} %fusion.10), channel_id=1, replica_groups=mesh['gx'=8,'gy'=4] {'gx','gy'}, use_global_device_ids=true, to_apply=%region_5.0 | all-reduce | flops 1 | bytes 8 | tf_op jit(solution)/shard_map/psum | solution.py:35
  360.8 3.0 fusion.14
  363.8 0.0 all-gather.7.cloned.1.call-start
  363.9 0.7 all-gather.7.cloned.1.call-update
  364.6 40.2 %all-gather.9.cloned.1.call-done = bf16[4608,576]{0,1:T(8,128)(2,1)} async-done(((bf16[1152,576]{0,1:T(8,128)(2,1)}), bf16[4608,576]{0,1:T(8,128)(2,1)}) %all-gather.9.cloned.1.call-update) | async-done | bytes 5308432 | tf_op jit(solution)/shard_map/all_gather | solution.py:40
  404.9 154.9 %all-gather.7.cloned.1.call-done = bf16[1152,4608]{0,1:T(8,128)(2,1)} async-done(((bf16[1152,576]{0,1:T(8,128)(2,1)}), bf16[1152,4608]{0,1:T(8,128)(2,1)}) %all-gather.7.cloned.1.call-update) | async-done | bytes 10616848 | tf_op jit(solution)/shard_map/all_gather | solution.py:41
  559.8 13.3 %fusion.15 = (bf16[1152,576]{0,1:T(8,128)(2,1)}, f32[1152,576]{0,1:T(8,128)}) fusion(bf16[4608,576]{0,1:T(8,128)(2,1)} %all-gather.9.cloned.1.call-done, bf16[1152,4608]{0,1:T(8,128)(2,1)} %all-gather.7.cloned.1.call-done), kind=kOutput, calls=%fused_computation.30 | convolution fusion | flops 6116622336 | bytes 19906560 | tf_op jit(solution)/shard_map/dot_general | solution.py:42
  573.1 0.2 all-gather.15.cloned.1.call-start
  573.4 38.9 %all-gather.11.cloned.1.call-done = bf16[4608,576]{0,1:T(8,128)(2,1)} async-done(((bf16[1152,576]{0,1:T(8,128)(2,1)}), bf16[4608,576]{0,1:T(8,128)(2,1)}) %all-gather.11.cloned.1.call-update) | async-done | bytes 5308432 | tf_op jit(solution)/shard_map/all_gather | solution.py:44
  612.2 12.9 %fusion.7 = bf16[1152,576]{0,1:T(8,128)(2,1)} fusion(bf16[4608,576]{0,1:T(8,128)(2,1)} %all-gather.11.cloned.1.call-done, bf16[1152,4608]{0,1:T(8,128)(2,1)} %all-gather.7.cloned.1.call-done, bf16[1152,576]{0,1:T(8,128)(2,1)S(1)} %copy-done.1), kind=kOutput, calls=%fused_computation.17 | convolution fusion | flops 6118612992 | bytes 18579456 | tf_op jit(solution)/shard_map/dot_general | solution.py:45
  625.1 0.0 all-gather.13.cloned.1.call-start
  625.2 0.5 all-gather.13.cloned.1.call-update
  625.7 0.0 all-gather.17.cloned.1.call-start
  625.7 40.3 %all-gather.15.cloned.1.call-done = bf16[4608,576]{0,1:T(8,128)(2,1)} async-done(((bf16[1152,576]{0,1:T(8,128)(2,1)}), bf16[4608,576]{0,1:T(8,128)(2,1)}) %all-gather.15.cloned.1.call-update) | async-done | bytes 5308432 | tf_op jit(solution)/shard_map/all_gather | solution.py:40
  666.0 154.8 %all-gather.13.cloned.1.call-done = bf16[1152,4608]{0,1:T(8,128)(2,1)} async-done(((bf16[1152,576]{0,1:T(8,128)(2,1)}), bf16[1152,4608]{0,1:T(8,128)(2,1)}) %all-gather.13.cloned.1.call-update) | async-done | bytes 10616848 | tf_op jit(solution)/shard_map/all_gather | solution.py:41
  820.8 14.1 %fusion.12 = (f32[]{:T(128)}, f32[]{:T(128)}, bf16[1152,576]{0,1:T(8,128)(2,1)}) fusion(f32[1152,576]{0,1:T(8,128)} %get-tuple-element.6, s32[1152]{0:T(1024)S(1)} %iota_add_fusion, s32[576]{0:T(1024)S(1)} %iota_add_fusion.1, bf16[4608,576]{0,1:T(8,128)(2,1)} %all-gather.15.cloned.1.call-done, bf16[1152,4608]{0,1:T(8,128)(2,1)} %all-gather.13.cloned.1.call-done), kind=kOutput, calls=%fused_computation.22 | convolution fusion | flops 6119940096 | bytes 19913480 | tf_op jit(solution)/shard_map/dot_general | solution.py:42
  834.9 1.4 pad_maximum_fusion
  836.3 39.1 %psum.31 = f32[2]{0:T(128)S(1)} all-reduce(f32[2]{0:T(128)S(1)} %pad_maximum_fusion), channel_id=1, replica_groups=mesh['gx'=8,'gy'=4] {'gx','gy'}, use_global_device_ids=true, to_apply=%region_8.0 | all-reduce | flops 2 | bytes 16 | tf_op jit(solution)/shard_map/psum | solution.py:48
  875.4 0.5 subtract_multiply_fusion
  875.9 12.9 %fusion.6 = bf16[1152,576]{0,1:T(8,128)(2,1)} fusion(bf16[4608,576]{0,1:T(8,128)(2,1)} %all-gather.17.cloned.1.call-done, bf16[1152,4608]{0,1:T(8,128)(2,1)} %all-gather.13.cloned.1.call-done, bf16[1152,576]{0,1:T(8,128)(2,1)S(1)} %copy-done.2), kind=kOutput, calls=%fused_computation.16 | convolution fusion | flops 6118612992 | bytes 18579456 | tf_op jit(solution)/shard_map/dot_general | solution.py:45
  (15 shorter events, 0.1 us)
Async XLA Ops:
  7.2 266.9 %reduce-scatter.2.cloned.1.call-start = ((), (), s32[]{:S(2)}) async-start(), calls=%async_computation.1 | async-start | bytes 11943936 | tf_op jit(solution)/shard_map/reduce_scatter | solution.py:18
  93.1 181.0 %copy-start = (f32[1152,576]{0,1:T(8,128)S(1)}, f32[1152,576]{0,1:T(8,128)}, u32[]{:S(2)}) copy-start(f32[1152,576]{0,1:T(8,128)} %param.5) | copy-start | bytes 7962628
  93.1 311.7 %all-gather.9.cloned.1.call-start = ((), (), s32[]{:S(2)}) async-start(), calls=%async_computation.3 | async-start | bytes 6635520 | tf_op jit(solution)/shard_map/all_gather | solution.py:40
  363.8 196.0 %all-gather.7.cloned.1.call-start = ((), (), s32[]{:S(2)}) async-start(), calls=%async_computation.2 | async-start | bytes 11943936 | tf_op jit(solution)/shard_map/all_gather | solution.py:41
  364.6 247.7 %copy-start.1 = (bf16[1152,576]{0,1:T(8,128)(2,1)S(1)}, bf16[1152,576]{0,1:T(8,128)(2,1)}, u32[]{:S(2)}) copy-start(bf16[1152,576]{0,1:T(8,128)(2,1)} %fusion.14) | copy-start | bytes 3981316
  364.6 247.6 %all-gather.11.cloned.1.call-start = ((), (), s32[]{:S(2)}) async-start(), calls=%async_computation.4 | async-start | bytes 6635520 | tf_op jit(solution)/shard_map/all_gather | solution.py:44
  573.1 92.9 %all-gather.15.cloned.1.call-start = ((), (), s32[]{:S(2)}) async-start(), calls=%async_computation.6 | async-start | bytes 6635520 | tf_op jit(solution)/shard_map/all_gather | solution.py:40
  625.1 195.7 %all-gather.13.cloned.1.call-start = ((), (), s32[]{:S(2)}) async-start(), calls=%async_computation.5 | async-start | bytes 11943936 | tf_op jit(solution)/shard_map/all_gather | solution.py:41
  625.7 250.2 %all-gather.17.cloned.1.call-start = ((), (), s32[]{:S(2)}) async-start(), calls=%async_computation.7 | async-start | bytes 6635520 | tf_op jit(solution)/shard_map/all_gather | solution.py:44
  820.8 55.1 %copy-start.2 = (bf16[1152,576]{0,1:T(8,128)(2,1)S(1)}, bf16[1152,576]{0,1:T(8,128)(2,1)}, u32[]{:S(2)}) copy-start(bf16[1152,576]{0,1:T(8,128)(2,1)} %fusion.7) | copy-start | bytes 3981316
Sparse Core Ops, SparseCore 0:
  93.3 180.7 reduce-scatter.1
  363.9 40.8 all-gather.8
  407.6 152.1 all-gather.6
  573.3 38.9 all-gather.10
  625.2 40.7 all-gather.14
  668.6 152.1 all-gather.12
  835.0 39.4 all-gather.16
where the time goes:
time: 897 us; the launch traced here: 896 us
  waiting for transfers between devices  611 us (68%)
  blocking collectives  128 us (14%)
  local copies, waits for them, and re-layouts  54.9 us (6%)
  matrix products  53.1 us (6%)
  other arithmetic  32 us (4%)
  between operations  16.2 us (2%)
    all_gather x2, waiting for transfers between devices, per_device(): row_panel = lax.all_gather(current, 'gx', axis=1, tiled=True)  310 us
    reduce_scatter x1, waiting for transfers between devices, per_device(): lax.psum_scatter(jnp.einsum('p,prc->cr', fitted16, three_index, preferred...  181 us
    all_gather x2, waiting for transfers between devices, per_device(): right = lax.all_gather(current, 'gy', axis=0, tiled=True)  80.5 us
    psum x1, blocking collectives, per_device(): lax.psum(jnp.sum(shifted * shifted), ('gx', 'gy')) / (width * width)  40.2 us
    psum x1, blocking collectives, per_device(): shift = lax.psum(local_trace, ('gx', 'gy')) / width  39.5 us
    psum x1, blocking collectives, per_device(): totals = lax.psum(jnp.stack(traces), ('gx', 'gy'))  39.1 us
    all_gather x2, waiting for transfers between devices, per_device(): square_block = lax.all_gather(square, 'gy', axis=0, tiled=True)  38.9 us
    dot_general x2, matrix products, per_device(): jnp.dot(row_panel, right, preferred_element_type=jnp.float32) * scale  27.4 us
  transfers between devices with their start and end apart: 7, of which 6 were waited for; matrix products, arithmetic and copies ran while one was open for 0% of the time, Pallas kernels for 0%

commit v1 on v0

--- a/solution.py
+++ b/solution.py
@@ -2,8 +2,15 @@
 import jax.numpy as jnp
 from jax import lax
 from jax.sharding import PartitionSpec as P
+from jax.lax import all_gather
 
 ITERS = 2
+
+
+def handle_cards(inner_x):
+    local_part = all_gather(inner_x, "gx")
+    earlier = jnp.concatenate(local_part, axis=1)
+    return earlier
 
 
 def per_device(three_index, old_density, core):
@@ -38,7 +45,7 @@
     traces = []
     for step in range(ITERS):
         right = lax.all_gather(current, "gy", axis=0, tiled=True)
-        row_panel = lax.all_gather(current, "gx", axis=1, tiled=True)
+        row_panel = handle_cards(current)
         square_full = jnp.dot(row_panel, right, preferred_element_type=jnp.float32) * scale
         square = square_full.astype(jnp.bfloat16)
         square_block = lax.all_gather(square, "gy", axis=0, tiled=True)

time: 897 us -> 895 us (level)
  waiting for transfers between devices: 611 us -> 588 us
  local copies, waits for them, and re-layouts: 54.9 us -> 74 us
    all_gather x0 -> x2, local copies, waits for them, and re-layouts: none -> 19.1 us  [handle_cards(): local_part = all_gather(inner_x, 'gx')]
    all_gather x2, waiting for transfers between devices: 80.5 us -> 62.9 us  [per_device(): right = lax.all_gather(current, 'gy', axis=0, tiled=True)]
  transfers between devices with their start and end apart: 7 -> 7, of which waited for: 6 -> 6; matrix products, arithmetic and copies ran while one was open for 0% -> 2% of each run, Pallas kernels for 0% -> 0%
where the time goes in v1:
time: 895 us; the launch traced here: 893 us
  waiting for transfers between devices  588 us (66%)
  blocking collectives  129 us (14%)
  local copies, waits for them, and re-layouts  74 us (8%)
  matrix products  53.2 us (6%)
  other arithmetic  31.9 us (4%)
  between operations  16.2 us (2%)
    all_gather x2, waiting for transfers between devices, handle_cards(): local_part = all_gather(inner_x, 'gx')  303 us
    reduce_scatter x1, waiting for transfers between devices, per_device(): lax.psum_scatter(jnp.einsum('p,prc->cr', fitted16, three_index, preferred...  181 us
    all_gather x2, waiting for transfers between devices, per_device(): right = lax.all_gather(current, 'gy', axis=0, tiled=True)  62.9 us
    all_gather x2, waiting for transfers between devices, per_device(): square_block = lax.all_gather(square, 'gy', axis=0, tiled=True)  40.7 us
    psum x1, blocking collectives, per_device(): lax.psum(jnp.sum(shifted * shifted), ('gx', 'gy')) / (width * width)  40.2 us
    psum x1, blocking collectives, per_device(): totals = lax.psum(jnp.stack(traces), ('gx', 'gy'))  40 us
    psum x1, blocking collectives, per_device(): shift = lax.psum(local_trace, ('gx', 'gy')) / width  39.5 us
    dot_general x2, matrix products, per_device(): jnp.dot(row_panel, right, preferred_element_type=jnp.float32) * scale  27.4 us
  transfers between devices with their start and end apart: 7, of which 6 were waited for; matrix products, arithmetic and copies ran while one was open for 2% of the time, Pallas kernels for 0%

profile of v1, /device:TPU:0, one launch (start us, length us, event | category | flops | bytes accessed | tf_op | source)
XLA Modules:
  0.0 892.6 jit_solution(8236411339931251218)
XLA Ops:
  7.2 19.8 %reshape.35 = bf16[5308416]{0:T(1024)(128)(2,1)} reshape(bf16[1,1152,4608]{2,1,0:T(8,128)(2,1)} %param.3) | data formatting | bytes 21233664 | tf_op jit(solution)/shard_map/reshape
  27.0 15.3 %copy.6 = bf16[1,1152,4608]{1,2,0:T(8,128)(2,1)} copy(bf16[1,1152,4608]{2,1,0:T(8,128)(2,1)} %param.3) | data formatting | bytes 21233664 | tf_op args[0]
  42.3 19.8 %reshape.36 = bf16[5308416]{0:T(1024)(128)(2,1)} reshape(bf16[1152,4608]{1,0:T(8,128)(2,1)} %param.4) | data formatting | bytes 21233664 | tf_op jit(solution)/shard_map/reshape | solution.py:21
  62.1 10.9 %fusion = f32[]{:T(128)} fusion(bf16[5308416]{0:T(1024)(128)(2,1)} %reshape.35, bf16[5308416]{0:T(1024)(128)(2,1)} %reshape.36), kind=kLoop, calls=%fused_computation.1 | loop fusion | flops 21233664 | bytes 21233668 | tf_op jit(solution)/shard_map/dot_general | solution.py:20
  72.9 9.0 %psum.28 = bf16[1]{0:T(256)(128)(2,1)} all-reduce(f32[1]{0:T(128)} %bitcast), channel_id=1, replica_groups=mesh['gx'=8,'gy'=4] {'gy'}, use_global_device_ids=true, to_apply=%region_0.0 | all-reduce | flops 1 | bytes 6 | tf_op jit(solution)/shard_map/psum | solution.py:23
  82.6 10.5 %fusion.1 = bf16[4608,1152]{1,0:T(8,128)(2,1)} fusion(bf16[1,1152,4608]{1,2,0:T(8,128)(2,1)} %copy.6, f32[]{:T(128)S(6)} %convert.13), kind=kLoop, calls=%fused_computation.3 | loop fusion | flops 15925248 | bytes 21233668 | tf_op jit(solution)/shard_map/convert_element_type | solution.py:26
  93.1 0.0 all-gather.17.cloned.1.call-start
  93.2 180.8 %reduce-scatter.2.cloned.1.call-done = bf16[576,1152]{1,0:T(8,128)(2,1)} async-done(((bf16[4608,1152]{1,0:T(8,128)(2,1)}), bf16[576,1152]{1,0:T(8,128)(2,1)}) %reduce-scatter.2.cloned.1.call-update) | async-done | bytes 1327120 | tf_op jit(solution)/shard_map/reduce_scatter | solution.py:25
  274.1 2.8 fusion.11
  276.9 39.5 %psum.29 = f32[]{:T(128)} all-reduce(f32[]{:T(128)} %fusion.11), channel_id=1, replica_groups=mesh['gx'=8,'gy'=4] {'gx','gy'}, use_global_device_ids=true, to_apply=%region_3.0 | all-reduce | flops 1 | bytes 8 | tf_op jit(solution)/shard_map/psum | solution.py:40
  317.0 2.9 fusion.10
  319.9 40.2 %psum.30 = f32[]{:T(128)} all-reduce(f32[]{:T(128)} %fusion.10), channel_id=1, replica_groups=mesh['gx'=8,'gy'=4] {'gx','gy'}, use_global_device_ids=true, to_apply=%region_5.0 | all-reduce | flops 1 | bytes 8 | tf_op jit(solution)/shard_map/psum | solution.py:42
  360.8 3.0 fusion.14
  363.8 0.0 all-gather.9.cloned.1.call-start
  363.9 0.7 all-gather.9.cloned.1.call-update
  364.6 151.2 %all-gather.17.cloned.1.call-done = bf16[9216,576]{0,1:T(8,128)(2,1)} async-done(((bf16[1152,576]{0,1:T(8,128)(2,1)}), bf16[9216,576]{0,1:T(8,128)(2,1)}) %all-gather.17.cloned.1.call-update) | async-done | bytes 10616848 | tf_op jit(solution)/shard_map/all_gather | solution.py:11
  515.9 9.6 %copy.17 = bf16[72,8,8,1152]{3,2,0,1:T(8,128)(2,1)} copy(bf16[72,8,8,1152]{3,2,1,0:T(8,128)(2,1)} %bitcast.43) | data formatting | bytes 21233664 | tf_op jit(solution)/shard_map/all_gather | solution.py:11
  525.4 31.6 %all-gather.9.cloned.1.call-done = bf16[4608,576]{0,1:T(8,128)(2,1)} async-done(((bf16[1152,576]{0,1:T(8,128)(2,1)}), bf16[4608,576]{0,1:T(8,128)(2,1)}) %all-gather.9.cloned.1.call-update) | async-done | bytes 5308432 | tf_op jit(solution)/shard_map/all_gather | solution.py:47
  557.0 13.4 %fusion.15 = (bf16[1152,576]{0,1:T(8,128)(2,1)}, f32[1152,576]{0,1:T(8,128)}) fusion(bf16[4608,576]{0,1:T(8,128)(2,1)} %all-gather.9.cloned.1.call-done, bf16[1152,4608]{0,1:T(8,128)(2,1)} %bitcast.41), kind=kOutput, calls=%fused_computation.32 | convolution fusion | flops 6116622336 | bytes 19906560 | tf_op jit(solution)/shard_map/dot_general | solution.py:49
  570.4 0.2 all-gather.19.cloned.1.call-start
  570.6 40.7 %all-gather.11.cloned.1.call-done = bf16[4608,576]{0,1:T(8,128)(2,1)} async-done(((bf16[1152,576]{0,1:T(8,128)(2,1)}), bf16[4608,576]{0,1:T(8,128)(2,1)}) %all-gather.11.cloned.1.call-update) | async-done | bytes 5308432 | tf_op jit(solution)/shard_map/all_gather | solution.py:51
  611.3 12.9 %fusion.7 = bf16[1152,576]{0,1:T(8,128)(2,1)} fusion(bf16[4608,576]{0,1:T(8,128)(2,1)} %all-gather.11.cloned.1.call-done, bf16[1152,4608]{0,1:T(8,128)(2,1)} %bitcast.42, bf16[1152,576]{0,1:T(8,128)(2,1)S(1)} %copy-done.1), kind=kOutput, calls=%fused_computation.19 | convolution fusion | flops 6118612992 | bytes 18579456 | tf_op jit(solution)/shard_map/dot_general | solution.py:52
  624.2 0.0 all-gather.13.cloned.1.call-start
  624.3 0.5 all-gather.13.cloned.1.call-update
  624.8 151.3 %all-gather.19.cloned.1.call-done = bf16[9216,576]{0,1:T(8,128)(2,1)} async-done(((bf16[1152,576]{0,1:T(8,128)(2,1)}), bf16[9216,576]{0,1:T(8,128)(2,1)}) %all-gather.19.cloned.1.call-update) | async-done | bytes 10616848 | tf_op jit(solution)/shard_map/all_gather | solution.py:11
  776.1 9.6 %copy.16 = bf16[72,8,8,1152]{3,2,0,1:T(8,128)(2,1)} copy(bf16[72,8,8,1152]{3,2,1,0:T(8,128)(2,1)} %bitcast.44) | data formatting | bytes 21233664 | tf_op jit(solution)/shard_map/all_gather | solution.py:11
  785.7 31.4 %all-gather.13.cloned.1.call-done = bf16[4608,576]{0,1:T(8,128)(2,1)} async-done(((bf16[1152,576]{0,1:T(8,128)(2,1)}), bf16[4608,576]{0,1:T(8,128)(2,1)}) %all-gather.13.cloned.1.call-update) | async-done | bytes 5308432 | tf_op jit(solution)/shard_map/all_gather | solution.py:47
  817.1 14.0 %fusion.12 = (f32[]{:T(128)}, f32[]{:T(128)}, bf16[1152,576]{0,1:T(8,128)(2,1)}) fusion(f32[1152,576]{0,1:T(8,128)} %get-tuple-element.6, s32[1152]{0:T(1024)S(1)} %iota_add_fusion, s32[576]{0:T(1024)S(1)} %iota_add_fusion.1, bf16[4608,576]{0,1:T(8,128)(2,1)} %all-gather.13.cloned.1.call-done, bf16[1152,4608]{0,1:T(8,128)(2,1)} %bitcast.39), kind=kOutput, calls=%fused_computation.24 | convolution fusion | flops 6119940096 | bytes 19913480 | tf_op jit(solution)/shard_map/dot_general | solution.py:49
  831.1 1.3 pad_maximum_fusion
  832.4 40.0 %psum.31 = f32[2]{0:T(128)S(1)} all-reduce(f32[2]{0:T(128)S(1)} %pad_maximum_fusion), channel_id=1, replica_groups=mesh['gx'=8,'gy'=4] {'gx','gy'}, use_global_device_ids=true, to_apply=%region_8.0 | all-reduce | flops 2 | bytes 16 | tf_op jit(solution)/shard_map/psum | solution.py:55
  872.4 0.5 subtract_multiply_fusion
  872.9 12.9 %fusion.6 = bf16[1152,576]{0,1:T(8,128)(2,1)} fusion(bf16[4608,576]{0,1:T(8,128)(2,1)} %all-gather.15.cloned.1.call-done, bf16[1152,4608]{0,1:T(8,128)(2,1)} %bitcast.40, bf16[1152,576]{0,1:T(8,128)(2,1)S(1)} %copy-done.2), kind=kOutput, calls=%fused_computation.18 | convolution fusion | flops 6118612992 | bytes 18579456 | tf_op jit(solution)/shard_map/dot_general | solution.py:52
  (17 shorter events, 0.2 us)
Async XLA Ops:
  7.2 266.9 %reduce-scatter.2.cloned.1.call-start = ((), (), s32[]{:S(2)}) async-start(), calls=%async_computation.1 | async-start | bytes 11943936 | tf_op jit(solution)/shard_map/reduce_scatter | solution.py:25
  93.1 181.0 %copy-start = (f32[1152,576]{0,1:T(8,128)S(1)}, f32[1152,576]{0,1:T(8,128)}, u32[]{:S(2)}) copy-start(f32[1152,576]{0,1:T(8,128)} %param.5) | copy-start | bytes 7962628
  93.1 422.7 %all-gather.17.cloned.1.call-start = ((), (), s32[]{:S(2)}) async-start(), calls=%async_computation.6 | async-start | bytes 11943936 | tf_op jit(solution)/shard_map/all_gather | solution.py:11
  363.8 193.1 %all-gather.9.cloned.1.call-start = ((), (), s32[]{:S(2)}) async-start(), calls=%async_computation.2 | async-start | bytes 6635520 | tf_op jit(solution)/shard_map/all_gather | solution.py:47
  364.6 246.8 %all-gather.11.cloned.1.call-start = ((), (), s32[]{:S(2)}) async-start(), calls=%async_computation.3 | async-start | bytes 6635520 | tf_op jit(solution)/shard_map/all_gather | solution.py:51
  557.0 54.4 %copy-start.1 = (bf16[1152,576]{0,1:T(8,128)(2,1)S(1)}, bf16[1152,576]{0,1:T(8,128)(2,1)}, u32[]{:S(2)}) copy-start(bf16[1152,576]{0,1:T(8,128)(2,1)} %fusion.14) | copy-start | bytes 3981316
  570.4 205.7 %all-gather.19.cloned.1.call-start = ((), (), s32[]{:S(2)}) async-start(), calls=%async_computation.7 | async-start | bytes 11943936 | tf_op jit(solution)/shard_map/all_gather | solution.py:11
  624.2 192.9 %all-gather.13.cloned.1.call-start = ((), (), s32[]{:S(2)}) async-start(), calls=%async_computation.4 | async-start | bytes 6635520 | tf_op jit(solution)/shard_map/all_gather | solution.py:47
  624.8 248.1 %all-gather.15.cloned.1.call-start = ((), (), s32[]{:S(2)}) async-start(), calls=%async_computation.5 | async-start | bytes 6635520 | tf_op jit(solution)/shard_map/all_gather | solution.py:51
  817.1 55.9 %copy-start.2 = (bf16[1152,576]{0,1:T(8,128)(2,1)S(1)}, bf16[1152,576]{0,1:T(8,128)(2,1)}, u32[]{:S(2)}) copy-start(bf16[1152,576]{0,1:T(8,128)(2,1)} %fusion.7) | copy-start | bytes 3981316
Sparse Core Ops, SparseCore 0:
  93.3 180.7 reduce-scatter.1
  363.9 151.8 all-gather.16
  518.0 38.9 all-gather.8
  570.5 40.7 all-gather.10
  624.3 151.7 all-gather.18
  778.1 38.9 all-gather.12
  831.2 41.4 all-gather.14
